TPU v7x, 32 devices: a whole 2x2x4 slice. The times are simulated.
32 devices in a mesh: rows: 2 (over y), cols: 4 (over z), slabs: 4 (over x, core).
Axes of the slice: x: 2, y: 2, z: 4, core: 2. Of those that a mesh axis runs over, the one named last changes fastest.
Arguments:
- field_values: float32 [8, 256, 256, 128], P('rows', 'cols', 'slabs'), may hold values from 0.2 to 1.8
- mobility: float32 [8, 256, 256, 128], P('rows', 'cols', 'slabs'), may hold values from 0.03 to 0.15
- source: float32 [8, 256, 256, 128], P('rows', 'cols', 'slabs'), may hold values from -0.2 to 0.2
Outputs:
- column_sum: float32 [8, 256, 256, 128], P('rows', 'cols', 'slabs')
- field_values_end: float32 [8, 256, 256, 128], P('rows', 'cols', 'slabs')
All inputs are finite; a program needn't handle non-finite values.
Results may differ from a plain program's by a relative error of at most 0.00002.
Values sent between devices are 32-bit elements; how exact they have to be, the bound alone decides.
A program may use at most 320 MiB of HBM per device.

v0:
```python
import jax
import jax.numpy as jnp
from jax import lax
from jax.sharding import PartitionSpec as P

STEPS = 4


def padded_2(array, sides, width):
    for axis, dim in sides:
        count, length = (lax.axis_size(axis), array.shape[dim])
        up = [(i, (i + 1) % count) for i in range(count - 1)]
        down = [(j, i) for i, j in up]
        last = lax.slice_in_dim(array, length - width, length, axis=dim)
        first = lax.slice_in_dim(array, 0, width, axis=dim)
        before = lax.ppermute(last, axis, up)
        after = lax.ppermute(first, axis, down)
        array = jnp.concatenate([before, array, after], axis=dim)
    return array


def prefix(array, axis, combine, identity):
    count, index = (lax.axis_size(axis), lax.axis_index(axis))
    everything = lax.all_gather(array, axis)
    start = jnp.broadcast_to(jnp.asarray(identity, array.dtype), array.shape)

    def lap(k, before):
        reached = k < index
        new = combine(before, everything[k])
        return jnp.where(reached, new, before)

    return lax.fori_loop(0, count, lap, start)


def strip_edges(values, dims):
    for dim in dims:
        values = lax.slice_in_dim(values, 1, values.shape[dim] - 1, axis=dim)
    return values


def neighbour(values, dim, start, dims):
    others = [other for other in dims if other != dim]
    values = strip_edges(values, others)
    return lax.slice_in_dim(values, start, start + values.shape[dim] - 2, axis=dim)


def one_step(padded, mobility, source):
    middle = strip_edges(padded, (0, 1, 2))
    lower = [neighbour(padded, dim, 0, (0, 1, 2)) for dim in (0, 1, 2)]
    upper = [neighbour(padded, dim, 2, (0, 1, 2)) for dim in (0, 1, 2)]
    spread = lower[0] + upper[0] + lower[1] + upper[1] + lower[2] + upper[2] - 6.0 * middle
    return middle + mobility * spread + source


def local(field_values, mobility, source):
    for step in range(STEPS):
        padded = padded_2(field_values, (("rows", 0), ("cols", 1), ("slabs", 2)), 1)
        field_values = one_step(padded, mobility, source)
    here = jnp.cumsum(field_values, axis=0)
    total = lax.slice_in_dim(here, here.shape[0] - 1, here.shape[0], axis=0)

    def add_pair(earlier_total, later_total):
        return earlier_total + later_total

    below = prefix(total, "rows", add_pair, jnp.zeros_like(total))
    column_sum = (here + below) / (field_values.shape[0] * lax.axis_size("rows"))
    return (column_sum, field_values)


def solution(mesh):
    in_specs = (
        P("rows", "cols", "slabs", None),
        P("rows", "cols", "slabs", None),
        P("rows", "cols", "slabs", None),
    )
    out_specs = (P("rows", "cols", "slabs", None), P("rows", "cols", "slabs", None))
    return jax.shard_map(local, mesh=mesh, in_specs=in_specs, out_specs=out_specs, check_vma=False)
```

profile of v0, /device:TPU:0, one launch (start us, length us, event | category | flops | bytes accessed | tf_op | source)
XLA Modules:
  0.0 498.0 jit_solution(8440209083768362149)
XLA Ops:
  7.2 4.1 fusion.40
  11.4 5.2 %collective-permute-start = (f32[1,64,64,128]{3,2,1,0:T(8,128)S(1)}, f32[1,64,64,128]{3,2,1,0:T(8,128)S(1)}, u32[]{:S(2)}, u32[]{:S(2)}) collective-permute-start(f32[1,64,64,128]{3,2,1,0:T(8,128)S(1)} %get-tuple-element.142), channel_id=1, source_target_pairs={{0,16},{1,17},{2,18},{3,19},{4,20},{5,21},{6,22},{7,23},{8,24},{9,... | collective-permute-start | bytes 6291464 | tf_op jit(solution)/shard_map/ppermute | solution.py:16
  17.8 43.4 %collective-permute-done = f32[1,64,64,128]{3,2,1,0:T(8,128)S(1)} collective-permute-done((f32[1,64,64,128]{3,2,1,0:T(8,128)S(1)}, f32[1,64,64,128]{3,2,1,0:T(8,128)S(1)}, u32[]{:S(2)}, u32[]{:S(2)}) %collective-permute-start) | collective-permute-done | bytes 2097184 | tf_op jit(solution)/shard_map/ppermute | solution.py:16
  62.8 1.7 constant_dynamic-update-slice_fusion.1
  65.8 1.7 constant_dynamic-update-slice_fusion
  67.6 3.8 collective-permute-start.2
  72.7 1.9 collective-permute-done.2
  74.5 4.4 collective-permute-done.3
  82.1 3.6 collective-permute-done.5
  85.9 26.7 %fusion.31 = f32[4,64,64,128]{3,2,1,0:T(8,128)S(1)} fusion(f32[4,64,64,128]{3,2,1,0:T(8,128)} %param.7, f32[4,64,64,128]{3,2,1,0:T(8,128)} %param.5, f32[4,64,64,128]{3,2,1,0:T(8,128)} %param.6, f32[6,66,1,128]{3,2,1,0:T(1,128)S(1)} %copy.29, f32[6,1,64,128]{3,2,1,0:T(8,128)S(1)} %collective-permute-done.3, f32[6,64,64,128]{3,2,1,0:T(8,128)} %copy-done.3, ...), kind=kLoop, calls=%fused_computation.87 | loop fusion | flops 41943040 | bytes 51130368 | tf_op jit(solution)/shard_map/add | solution.py:52
  113.2 3.2 collective-permute-start.6
  117.7 41.2 %collective-permute-done.6 = f32[1,64,64,128]{3,2,1,0:T(8,128)S(1)} collective-permute-done((f32[1,64,64,128]{3,2,1,0:T(8,128)S(1)}, f32[1,64,64,128]{3,2,1,0:T(8,128)S(1)}, u32[]{:S(2)}, u32[]{:S(2)}) %collective-permute-start.6) | collective-permute-done | bytes 2097184 | tf_op jit(solution)/shard_map/ppermute | solution.py:16
  158.8 4.8 collective-permute-done.7
  163.7 3.5 collective-permute-start.8
  168.5 2.0 collective-permute-done.8
  170.5 4.7 collective-permute-done.9
  175.5 3.4 collective-permute-start.10
  178.9 1.5 collective-permute-start.11
  180.7 1.8 collective-permute-done.11
  182.6 28.6 %fusion.22 = f32[4,64,64,128]{3,2,1,0:T(8,128)} fusion(f32[4,64,64,128]{3,2,1,0:T(8,128)} %param.7, f32[4,64,64,128]{3,2,1,0:T(8,128)} %copy-done, f32[4,64,64,128]{3,2,1,0:T(8,128)} %param.6, f32[6,66,1,128]{3,2,1,0:T(1,128)S(1)} %copy.33, f32[6,1,64,128]{3,2,1,0:T(8,128)S(1)} %collective-permute-done.9, f32[6,1,64,128]{3,2,1,0:T(8,128)S(1)} %collective-permute-done.8, ...), kind=kLoop, calls=%fused_computation.60 | loop fusion | flops 58720256 | bytes 38547456 | tf_op jit(solution)/shard_map/add | solution.py:52
  211.3 2.7 fusion.38
  214.0 1.8 collective-permute-start.12
  217.1 41.0 %collective-permute-done.12 = f32[1,64,64,128]{3,2,1,0:T(8,128)S(1)} collective-permute-done((f32[1,64,64,128]{3,2,1,0:T(8,128)S(1)}, f32[1,64,64,128]{3,2,1,0:T(8,128)S(1)}, u32[]{:S(2)}, u32[]{:S(2)}) %collective-permute-start.12) | collective-permute-done | bytes 2097184 | tf_op jit(solution)/shard_map/ppermute | solution.py:16
  258.2 4.8 collective-permute-done.13
  263.0 3.5 collective-permute-start.14
  267.8 1.9 collective-permute-done.14
  269.7 4.7 collective-permute-done.15
  274.6 3.6 collective-permute-start.16
  279.8 2.2 collective-permute-done.17
  282.2 28.6 %fusion.13 = f32[4,64,64,128]{3,2,1,0:T(8,128)} fusion(f32[4,64,64,128]{3,2,1,0:T(8,128)} %param.7, f32[4,64,64,128]{3,2,1,0:T(8,128)} %fusion.22, f32[4,64,64,128]{3,2,1,0:T(8,128)} %param.6, f32[6,66,1,128]{3,2,1,0:T(1,128)S(1)} %copy.37, f32[6,1,64,128]{3,2,1,0:T(8,128)S(1)} %collective-permute-done.15, f32[6,1,64,128]{3,2,1,0:T(8,128)S(1)} %collective-permute-done.14, ...), kind=kLoop, calls=%fused_computation.33 | loop fusion | flops 58720256 | bytes 38547456 | tf_op jit(solution)/shard_map/add | solution.py:52
  310.8 2.7 fusion.37
  313.5 1.8 collective-permute-start.18
  316.7 41.0 %collective-permute-done.18 = f32[1,64,64,128]{3,2,1,0:T(8,128)S(1)} collective-permute-done((f32[1,64,64,128]{3,2,1,0:T(8,128)S(1)}, f32[1,64,64,128]{3,2,1,0:T(8,128)S(1)}, u32[]{:S(2)}, u32[]{:S(2)}) %collective-permute-start.18) | collective-permute-done | bytes 2097184 | tf_op jit(solution)/shard_map/ppermute | solution.py:16
  357.7 4.8 collective-permute-done.19
  362.5 1.9 collective-permute-start.20
  365.8 1.9 collective-permute-done.20
  367.6 4.7 collective-permute-done.21
  372.6 3.6 collective-permute-start.22
  376.2 1.5 collective-permute-start.23
  378.0 2.0 collective-permute-done.23
  380.2 28.6 %fusion.4 = f32[4,64,64,128]{3,2,1,0:T(8,128)} fusion(f32[4,64,64,128]{3,2,1,0:T(8,128)} %param.7, f32[4,64,64,128]{3,2,1,0:T(8,128)} %fusion.13, f32[4,64,64,128]{3,2,1,0:T(8,128)} %param.6, f32[6,66,1,128]{3,2,1,0:T(1,128)S(1)} %copy.41, f32[6,1,64,128]{3,2,1,0:T(8,128)S(1)} %collective-permute-done.21, f32[6,1,64,128]{3,2,1,0:T(8,128)S(1)} %collective-permute-done.20, ...), kind=kLoop, calls=%fused_computation.6 | loop fusion | flops 58720256 | bytes 38547456 | tf_op jit(solution)/shard_map/add | solution.py:52
  408.8 8.7 %fusion.41 = f32[4,64,64,128]{3,2,1,0:T(8,128)} fusion(f32[4,64,64,128]{3,2,1,0:T(8,128)} %fusion.4), kind=kOutput, calls=%fused_computation.137 | output fusion | flops 6291456 | bytes 16777216 | tf_op jit(solution)/shard_map/jit(cumsum)/reduce_window_sum | solution.py:59
  417.5 3.2 slice.360
  420.7 57.0 %all-gather.3.cloned.1.call-done = f32[2,64,64,128]{3,2,1,0:T(8,128)} async-done(((f32[1,64,64,128]{3,2,1,0:T(8,128)}), f32[2,64,64,128]{3,2,1,0:T(8,128)}) %all-gather.3.cloned.1.call-update) | async-done | bytes 4194320 | tf_op jit(solution)/shard_map/all_gather | solution.py:24
  477.7 4.6 while.14
  477.7 2.3 add_select_fusion.2
  480.1 2.3 add_select_fusion.2
  482.4 8.8 %add_multiply_fusion = f32[4,64,64,128]{3,2,1,0:T(8,128)} fusion(f32[4,64,64,128]{3,2,1,0:T(8,128)} %fusion.41, f32[64,64,128]{2,1,0:T(8,128)S(1)} %bitcast.9), kind=kLoop, calls=%fused_computation.101 | loop fusion | flops 4194304 | bytes 18874368 | tf_op jit(solution)/shard_map/div | solution.py:66
  (65 shorter events, 20.8 us)
Async XLA Ops:
  7.2 470.6 %all-gather.3.cloned.1.call-start = ((), (), s32[]{:S(2)}) async-start(), calls=%async_computation | async-start | bytes 6291456 | tf_op jit(solution)/shard_map/all_gather | solution.py:24
  7.2 55.6 %copy-start.4 = (f32[4,64,64,128]{3,2,1,0:T(8,128)S(1)}, f32[4,64,64,128]{3,2,1,0:T(8,128)}, u32[]{:S(2)}) copy-start(f32[4,64,64,128]{3,2,1,0:T(8,128)} %param.5) | copy-start | bytes 25165828
  11.4 49.9 %collective-permute-start = (f32[1,64,64,128]{3,2,1,0:T(8,128)S(1)}, f32[1,64,64,128]{3,2,1,0:T(8,128)S(1)}, u32[]{:S(2)}, u32[]{:S(2)}) collective-permute-start(f32[1,64,64,128]{3,2,1,0:T(8,128)S(1)} %get-tuple-element.142), channel_id=1, source_target_pairs={{0,16},{1,17},{2,18},{3,19},{4,20},{5,21},{6,22},{7,23},{8,24},{9,... | collective-permute-start | bytes 6291464 | tf_op jit(solution)/shard_map/ppermute | solution.py:16
  16.5 49.3 %collective-permute-start.1 = (f32[1,64,64,128]{3,2,1,0:T(8,128)}, f32[1,64,64,128]{3,2,1,0:T(8,128)}, u32[]{:S(2)}, u32[]{:S(2)}) collective-permute-start(f32[1,64,64,128]{3,2,1,0:T(8,128)} %get-tuple-element.141), channel_id=1, source_target_pairs={{16,0},{17,1},{18,2},{19,3},{20,4},{21,5},{22,6},{23,7},{24,8},{25... | collective-permute-start | bytes 6291464 | tf_op jit(solution)/shard_map/ppermute | solution.py:17
  61.3 1.3 copy-start.8
  67.6 18.1 %copy-start.3 = (f32[6,64,64,128]{3,2,1,0:T(8,128)}, f32[6,64,64,128]{3,2,1,0:T(8,128)S(1)}, u32[]{:S(2)}) copy-start(f32[6,64,64,128]{3,2,1,0:T(8,128)S(1)} %constant_dynamic-update-slice_fusion) | copy-start | bytes 37748740
  67.6 18.3 %copy-start.9 = (f32[1,64,64,128]{3,2,1,0:T(8,128)S(1)}, f32[1,64,64,128]{3,2,1,0:T(8,128)}, u32[]{:S(2)}) copy-start(f32[1,64,64,128]{3,2,1,0:T(8,128)} %copy-done.8) | copy-start | bytes 6291460
  67.6 6.9 %collective-permute-start.2 = (f32[6,1,64,128]{3,2,1,0:T(8,128)S(1)}, f32[6,1,64,128]{3,2,1,0:T(8,128)S(1)}, u32[]{:S(2)}, u32[]{:S(2)}) collective-permute-start(f32[6,1,64,128]{3,2,1,0:T(8,128)S(1)} %get-tuple-element.133), channel_id=1, source_target_pairs={{0,4},{4,8},{8,12},{1,5},{5,9},{9,13},{2,6},{6,10},{10,14},{3,7},{... | collective-permute-start | bytes 589832 | tf_op jit(solution)/shard_map/ppermute | solution.py:16
  71.4 7.6 %collective-permute-start.3 = (f32[6,1,64,128]{3,2,1,0:T(8,128)S(1)}, f32[6,1,64,128]{3,2,1,0:T(8,128)S(1)}, u32[]{:S(2)}, u32[]{:S(2)}) collective-permute-start(f32[6,1,64,128]{3,2,1,0:T(8,128)S(1)} %get-tuple-element.134), channel_id=1, source_target_pairs={{4,0},{8,4},{12,8},{5,1},{9,5},{13,9},{6,2},{10,6},{14,10},{7,3},{... | collective-permute-start | bytes 589832 | tf_op jit(solution)/shard_map/ppermute | solution.py:17
  79.3 2.6 collective-permute-start.4
  80.6 5.1 %collective-permute-start.5 = (f32[6,66,1,128]{3,1,2,0:T(8,128)S(1)}, f32[6,66,1,128]{3,1,2,0:T(8,128)S(1)}, u32[]{:S(2)}, u32[]{:S(2)}) collective-permute-start(f32[6,66,1,128]{3,1,2,0:T(8,128)S(1)} %copy.28), channel_id=1, source_target_pairs={{1,0},{2,1},{3,2},{5,4},{6,5},{7,6},{9,8},{10,9},{11,10},{13,12},{... | collective-permute-start | bytes 608264 | tf_op jit(solution)/shard_map/ppermute | solution.py:17
  112.6 62.5 %copy-start = (f32[4,64,64,128]{3,2,1,0:T(8,128)}, f32[4,64,64,128]{3,2,1,0:T(8,128)S(1)}, u32[]{:S(2)}) copy-start(f32[4,64,64,128]{3,2,1,0:T(8,128)S(1)} %fusion.31) | copy-start | bytes 25165828
  113.2 45.7 %collective-permute-start.6 = (f32[1,64,64,128]{3,2,1,0:T(8,128)S(1)}, f32[1,64,64,128]{3,2,1,0:T(8,128)S(1)}, u32[]{:S(2)}, u32[]{:S(2)}) collective-permute-start(f32[1,64,64,128]{3,2,1,0:T(8,128)S(1)} %get-tuple-element.139), channel_id=1, source_target_pairs={{0,16},{1,17},{2,18},{3,19},{4,20},{5,21},{6,22},{7,23},{8,24},{9,... | collective-permute-start | bytes 6291464 | tf_op jit(solution)/shard_map/ppermute | solution.py:16
  116.4 47.3 %collective-permute-start.7 = (f32[1,64,64,128]{3,2,1,0:T(8,128)S(1)}, f32[1,64,64,128]{3,2,1,0:T(8,128)S(1)}, u32[]{:S(2)}, u32[]{:S(2)}) collective-permute-start(f32[1,64,64,128]{3,2,1,0:T(8,128)S(1)} %get-tuple-element.140), channel_id=1, source_target_pairs={{16,0},{17,1},{18,2},{19,3},{20,4},{21,5},{22,6},{23,7},{24,8},{25... | collective-permute-start | bytes 6291464 | tf_op jit(solution)/shard_map/ppermute | solution.py:17
  163.7 11.8 %copy-start.5 = (f32[1,64,64,128]{3,2,1,0:T(8,128)}, f32[1,64,64,128]{3,2,1,0:T(8,128)S(1)}, u32[]{:S(2)}) copy-start(f32[1,64,64,128]{3,2,1,0:T(8,128)S(1)} %collective-permute-done.7) | copy-start | bytes 6291460
  163.7 6.8 %collective-permute-start.8 = (f32[6,1,64,128]{3,2,1,0:T(8,128)S(1)}, f32[6,1,64,128]{3,2,1,0:T(8,128)S(1)}, u32[]{:S(2)}, u32[]{:S(2)}) collective-permute-start(f32[6,1,64,128]{3,2,1,0:T(8,128)S(1)} %get-tuple-element.131), channel_id=1, source_target_pairs={{0,4},{4,8},{8,12},{1,5},{5,9},{9,13},{2,6},{6,10},{10,14},{3,7},{... | collective-permute-start | bytes 589832 | tf_op jit(solution)/shard_map/ppermute | solution.py:16
  167.2 8.0 %collective-permute-start.9 = (f32[6,1,64,128]{3,2,1,0:T(8,128)S(1)}, f32[6,1,64,128]{3,2,1,0:T(8,128)S(1)}, u32[]{:S(2)}, u32[]{:S(2)}) collective-permute-start(f32[6,1,64,128]{3,2,1,0:T(8,128)S(1)} %get-tuple-element.132), channel_id=1, source_target_pairs={{4,0},{8,4},{12,8},{5,1},{9,5},{13,9},{6,2},{10,6},{14,10},{7,3},{... | collective-permute-start | bytes 589832 | tf_op jit(solution)/shard_map/ppermute | solution.py:17
  175.5 5.0 collective-permute-start.10
  178.9 3.5 collective-permute-start.11
  211.3 51.7 %copy-start.1 = (f32[4,64,64,128]{3,2,1,0:T(8,128)S(1)}, f32[4,64,64,128]{3,2,1,0:T(8,128)}, u32[]{:S(2)}) copy-start(f32[4,64,64,128]{3,2,1,0:T(8,128)} %fusion.22) | copy-start | bytes 25165828
  214.0 44.2 %collective-permute-start.12 = (f32[1,64,64,128]{3,2,1,0:T(8,128)S(1)}, f32[1,64,64,128]{3,2,1,0:T(8,128)S(1)}, u32[]{:S(2)}, u32[]{:S(2)}) collective-permute-start(f32[1,64,64,128]{3,2,1,0:T(8,128)S(1)} %get-tuple-element.137), channel_id=1, source_target_pairs={{0,16},{1,17},{2,18},{3,19},{4,20},{5,21},{6,22},{7,23},{8,24},{9,... | collective-permute-start | bytes 6291464 | tf_op jit(solution)/shard_map/ppermute | solution.py:16
  215.8 47.1 %collective-permute-start.13 = (f32[1,64,64,128]{3,2,1,0:T(8,128)S(1)}, f32[1,64,64,128]{3,2,1,0:T(8,128)S(1)}, u32[]{:S(2)}, u32[]{:S(2)}) collective-permute-start(f32[1,64,64,128]{3,2,1,0:T(8,128)S(1)} %get-tuple-element.138), channel_id=1, source_target_pairs={{16,0},{17,1},{18,2},{19,3},{20,4},{21,5},{22,6},{23,7},{24,8},{25... | collective-permute-start | bytes 6291464 | tf_op jit(solution)/shard_map/ppermute | solution.py:17
  263.0 11.6 %copy-start.6 = (f32[1,64,64,128]{3,2,1,0:T(8,128)}, f32[1,64,64,128]{3,2,1,0:T(8,128)S(1)}, u32[]{:S(2)}) copy-start(f32[1,64,64,128]{3,2,1,0:T(8,128)S(1)} %collective-permute-done.13) | copy-start | bytes 6291460
  263.0 6.7 %collective-permute-start.14 = (f32[6,1,64,128]{3,2,1,0:T(8,128)S(1)}, f32[6,1,64,128]{3,2,1,0:T(8,128)S(1)}, u32[]{:S(2)}, u32[]{:S(2)}) collective-permute-start(f32[6,1,64,128]{3,2,1,0:T(8,128)S(1)} %get-tuple-element.129), channel_id=1, source_target_pairs={{0,4},{4,8},{8,12},{1,5},{5,9},{9,13},{2,6},{6,10},{10,14},{3,7},{... | collective-permute-start | bytes 589832 | tf_op jit(solution)/shard_map/ppermute | solution.py:16
  266.5 7.8 %collective-permute-start.15 = (f32[6,1,64,128]{3,2,1,0:T(8,128)S(1)}, f32[6,1,64,128]{3,2,1,0:T(8,128)S(1)}, u32[]{:S(2)}, u32[]{:S(2)}) collective-permute-start(f32[6,1,64,128]{3,2,1,0:T(8,128)S(1)} %get-tuple-element.130), channel_id=1, source_target_pairs={{4,0},{8,4},{12,8},{5,1},{9,5},{13,9},{6,2},{10,6},{14,10},{7,3},{... | collective-permute-start | bytes 589832 | tf_op jit(solution)/shard_map/ppermute | solution.py:17
  274.6 4.9 collective-permute-start.16
  278.3 3.7 collective-permute-start.17
  310.8 51.7 %copy-start.2 = (f32[4,64,64,128]{3,2,1,0:T(8,128)S(1)}, f32[4,64,64,128]{3,2,1,0:T(8,128)}, u32[]{:S(2)}) copy-start(f32[4,64,64,128]{3,2,1,0:T(8,128)} %fusion.13) | copy-start | bytes 25165828
  313.5 44.2 %collective-permute-start.18 = (f32[1,64,64,128]{3,2,1,0:T(8,128)S(1)}, f32[1,64,64,128]{3,2,1,0:T(8,128)S(1)}, u32[]{:S(2)}, u32[]{:S(2)}) collective-permute-start(f32[1,64,64,128]{3,2,1,0:T(8,128)S(1)} %get-tuple-element.135), channel_id=1, source_target_pairs={{0,16},{1,17},{2,18},{3,19},{4,20},{5,21},{6,22},{7,23},{8,24},{9,... | collective-permute-start | bytes 6291464 | tf_op jit(solution)/shard_map/ppermute | solution.py:16
  315.4 47.1 %collective-permute-start.19 = (f32[1,64,64,128]{3,2,1,0:T(8,128)S(1)}, f32[1,64,64,128]{3,2,1,0:T(8,128)S(1)}, u32[]{:S(2)}, u32[]{:S(2)}) collective-permute-start(f32[1,64,64,128]{3,2,1,0:T(8,128)S(1)} %get-tuple-element.136), channel_id=1, source_target_pairs={{16,0},{17,1},{18,2},{19,3},{20,4},{21,5},{22,6},{23,7},{24,8},{25... | collective-permute-start | bytes 6291464 | tf_op jit(solution)/shard_map/ppermute | solution.py:17
  362.5 10.1 %copy-start.7 = (f32[1,64,64,128]{3,2,1,0:T(8,128)}, f32[1,64,64,128]{3,2,1,0:T(8,128)S(1)}, u32[]{:S(2)}) copy-start(f32[1,64,64,128]{3,2,1,0:T(8,128)S(1)} %collective-permute-done.19) | copy-start | bytes 6291460
  362.5 5.1 %collective-permute-start.20 = (f32[6,1,64,128]{3,2,1,0:T(8,128)S(1)}, f32[6,1,64,128]{3,2,1,0:T(8,128)S(1)}, u32[]{:S(2)}, u32[]{:S(2)}) collective-permute-start(f32[6,1,64,128]{3,2,1,0:T(8,128)S(1)} %get-tuple-element.127), channel_id=1, source_target_pairs={{0,4},{4,8},{8,12},{1,5},{5,9},{9,13},{2,6},{6,10},{10,14},{3,7},{... | collective-permute-start | bytes 589832 | tf_op jit(solution)/shard_map/ppermute | solution.py:16
  364.5 7.8 %collective-permute-start.21 = (f32[6,1,64,128]{3,2,1,0:T(8,128)S(1)}, f32[6,1,64,128]{3,2,1,0:T(8,128)S(1)}, u32[]{:S(2)}, u32[]{:S(2)}) collective-permute-start(f32[6,1,64,128]{3,2,1,0:T(8,128)S(1)} %get-tuple-element.128), channel_id=1, source_target_pairs={{4,0},{8,4},{12,8},{5,1},{9,5},{13,9},{6,2},{10,6},{14,10},{7,3},{... | collective-permute-start | bytes 589832 | tf_op jit(solution)/shard_map/ppermute | solution.py:17
  372.6 5.1 %collective-permute-start.22 = (f32[6,66,1,128]{3,1,2,0:T(8,128)S(1)}, f32[6,66,1,128]{3,1,2,0:T(8,128)S(1)}, u32[]{:S(2)}, u32[]{:S(2)}) collective-permute-start(f32[6,66,1,128]{3,1,2,0:T(8,128)S(1)} %copy.38), channel_id=1, source_target_pairs={{0,1},{1,2},{2,3},{4,5},{5,6},{6,7},{8,9},{9,10},{10,11},{12,13},{... | collective-permute-start | bytes 608264 | tf_op jit(solution)/shard_map/ppermute | solution.py:16
  376.2 3.7 collective-permute-start.23
Sparse Core Ops, SparseCore 0:
  420.8 56.8 all-gather.2
where the time goes:
time: 499 us; the launch traced here: 498 us
  waiting for transfers between devices  275 us (55%)
  other arithmetic  136 us (27%)
  starting transfers between devices  52.5 us (11%)
  local copies, waits for them, and re-layouts  20.1 us (4%)
  between operations  14.6 us (3%)
    ppermute x12, waiting for transfers between devices, padded_2(): before = lax.ppermute(last, axis, up)  174 us
    add x4, other arithmetic, one_step(): return middle + mobility * spread + source  113 us
    all_gather x1, waiting for transfers between devices, prefix(): everything = lax.all_gather(array, axis)  57 us
    ppermute x12, waiting for transfers between devices, padded_2(): after = lax.ppermute(first, axis, down)  43.7 us
    ppermute x12, starting transfers between devices, padded_2(): before = lax.ppermute(last, axis, up)  36.6 us
    ppermute x12, starting transfers between devices, padded_2(): after = lax.ppermute(first, axis, down)  15.9 us
  transfers between devices with their start and end apart: 25, of which 21 were waited for; matrix products, arithmetic and copies ran while one was open for 1% of the time, Pallas kernels for 0%

commit v1 on v0

--- a/solution.py
+++ b/solution.py
@@ -1,9 +1,332 @@
+import functools
+import math
+
 import jax
 import jax.numpy as jnp
 from jax import lax
+from jax.experimental import pallas as pl
+from jax.experimental.pallas import tpu as pltpu
 from jax.sharding import PartitionSpec as P
 
 STEPS = 4
+MESH = pl.DeviceIdType.MESH
+
+
+def kernel(counts, chunk, f_in, m_in, s_in, cs_out, f_out, fb, mb, sb, rhalo, khalo, ksend, row_send, row_recv, i_send, i_recv, k_send, k_recv, load_sem, out_sem):
+    n_rows, n_cols, n_slabs = counts
+    nj, ni, nk, lanes = f_in.shape
+    n_chunks = ni // chunk
+    scale = 1.0 / (nj * n_rows)
+    r, c, s = (lax.axis_index(name) for name in ("rows", "cols", "slabs"))
+    up, down, left, right = c > 0, c < n_cols - 1, s > 0, s < n_slabs - 1
+    edge = jnp.where(r == 0, nj - 1, 0)
+    is_low = (r == 0).astype(jnp.float32)
+    is_high = (r == 1).astype(jnp.float32)
+    peer = {"rows": 1 - r}
+    beside = (
+        (up, {"cols": c - 1}),
+        (down, {"cols": c + 1}),
+        (left, {"slabs": s - 1}),
+        (right, {"slabs": s + 1}),
+    )
+
+    loads = [
+        pltpu.make_async_copy(f_in, fb.at[0, :, pl.ds(1, ni)], load_sem.at[0]),
+        pltpu.make_async_copy(m_in, mb, load_sem.at[1]),
+        pltpu.make_async_copy(s_in, sb, load_sem.at[2]),
+    ]
+    for load in loads:
+        load.start()
+
+    barrier = pltpu.get_barrier_semaphore()
+    pl.semaphore_signal(barrier, inc=1, device_id=peer, device_id_type=MESH)
+    for there, device in beside:
+
+        @pl.when(there)
+        def _(device=device):
+            pl.semaphore_signal(barrier, inc=1, device_id=device, device_id_type=MESH)
+
+    arrivals = 1 + sum(there.astype(jnp.int32) for there, _ in beside)
+    pl.semaphore_wait(barrier, arrivals)
+
+    def rows_of(k):
+        return pl.ds(k * chunk, chunk)
+
+    def remote(src, dst, send, recv, device):
+        return pltpu.make_async_remote_copy(src_ref=src, dst_ref=dst, send_sem=send, recv_sem=recv, device_id=device, device_id_type=MESH)
+
+    def row_copy(src, t, k):
+        return remote(src, rhalo.at[t, rows_of(k)], row_send.at[t, k], row_recv.at[t, k], peer)
+
+    def boundary(t, k):
+        return fb.at[lax.rem(t, 2), edge, pl.ds(1 + k * chunk, chunk)]
+
+    def i_first(t, src=None):
+        p = lax.rem(t, 2)
+        src = fb.at[p, :, 1] if src is None else src
+        return remote(src, fb.at[p, :, ni + 1], i_send.at[t, 0], i_recv.at[t, 1], {"cols": c - 1})
+
+    def i_last(t, src=None):
+        p = lax.rem(t, 2)
+        src = fb.at[p, :, ni] if src is None else src
+        return remote(src, fb.at[p, :, 0], i_send.at[t, 1], i_recv.at[t, 0], {"cols": c + 1})
+
+    def k_first(t):
+        return remote(ksend.at[t, 0], khalo.at[t, 1], k_send.at[t, 0], k_recv.at[t, 1], {"slabs": s - 1})
+
+    def k_last(t):
+        return remote(ksend.at[t, 1], khalo.at[t, 0], k_send.at[t, 1], k_recv.at[t, 0], {"slabs": s + 1})
+
+    def first_send(k, carry):
+        row_copy(f_in.at[edge, rows_of(k)], 0, k).start()
+        return carry
+
+    lax.fori_loop(0, n_chunks, first_send, 0)
+
+    @pl.when(up)
+    def _():
+        i_first(0, f_in.at[:, 0]).start()
+
+    @pl.when(down)
+    def _():
+        i_last(0, f_in.at[:, ni - 1]).start()
+
+    for there, place in ((up, 0), (down, ni + 1)):
+
+        @pl.when(jnp.logical_not(there))
+        def _(place=place):
+            for p in range(2):
+                fb[p, :, place] = jnp.zeros((nj, nk, lanes), jnp.float32)
+
+    for there, side in ((left, 0), (right, 1)):
+
+        @pl.when(jnp.logical_not(there))
+        def _(side=side):
+            def clear(t, carry):
+                khalo[t, side] = jnp.zeros((nj, ni, lanes), jnp.float32)
+                return carry
+
+            lax.fori_loop(0, STEPS, clear, 0)
+
+    loads[0].wait()
+
+    def first_edges(i, carry):
+        for j in range(nj):
+            ksend[0, 0, j, pl.ds(i, 1), :] = fb[0, j, i + 1, 0:1, :]
+            ksend[0, 1, j, pl.ds(i, 1), :] = fb[0, j, i + 1, nk - 1 : nk, :]
+        return carry
+
+    lax.fori_loop(0, ni, first_edges, 0)
+
+    def send_k(t):
+        @pl.when(left)
+        def _():
+            k_first(t).start()
+
+        @pl.when(right)
+        def _():
+            k_last(t).start()
+
+    send_k(0)
+    loads[1].wait()
+    loads[2].wait()
+
+    place = lax.broadcasted_iota(jnp.int32, (nk, lanes), 0)
+    at_first, at_last = place == 0, place == nk - 1
+
+    def step_chunk(t, k, final):
+        p = lax.rem(t, 2)
+        q = 1 - p
+        row_copy(boundary(t, k), t, k).wait_recv()
+
+        @pl.when(jnp.logical_and(k == 0, up))
+        def _():
+            i_last(t).wait_recv()
+
+        @pl.when(jnp.logical_and(k == 0, left))
+        def _():
+            k_last(t).wait_recv()
+
+        @pl.when(jnp.logical_and(k == 0, right))
+        def _():
+            k_first(t).wait_recv()
+
+        @pl.when(jnp.logical_and(k == n_chunks - 1, down))
+        def _():
+            i_first(t).wait_recv()
+
+        @pl.when(t >= 1)
+        def _():
+            row_copy(boundary(t - 1, k), t - 1, k).wait_send()
+
+        @pl.when(jnp.logical_and(t >= 1, jnp.logical_and(k == 0, up)))
+        def _():
+            i_first(t - 1).wait_send()
+
+        @pl.when(jnp.logical_and(t >= 1, jnp.logical_and(k == n_chunks - 1, down)))
+        def _():
+            i_last(t - 1).wait_send()
+
+        def one_row(n, carry):
+            i = k * chunk + n
+            halo = rhalo[t, i]
+            total = None
+            for j in range(nj):
+                x = fb[p, j, i + 1]
+                before = fb[p, j - 1, i + 1] if j > 0 else halo * is_high
+                after = fb[p, j + 1, i + 1] if j < nj - 1 else halo * is_low
+                k_before = jnp.where(at_first, khalo[t, 0, j, pl.ds(i, 1), :], pltpu.roll(x, 1, 0))
+                k_after = jnp.where(at_last, khalo[t, 1, j, pl.ds(i, 1), :], pltpu.roll(x, nk - 1, 0))
+                spread = before + after + fb[p, j, i] + fb[p, j, i + 2] + k_before + k_after - 6.0 * x
+                new = x + mb[j, i] * spread + sb[j, i]
+                fb[q, j, i + 1] = new
+                if final:
+                    total = new if total is None else total + new
+                    sb[j, i] = total * scale
+                else:
+                    ksend[t + 1, 0, j, pl.ds(i, 1), :] = new[0:1]
+                    ksend[t + 1, 1, j, pl.ds(i, 1), :] = new[nk - 1 : nk]
+            return carry
+
+        lax.fori_loop(0, chunk, one_row, 0)
+
+    def step(t, carry):
+        def lap(k, carry):
+            step_chunk(t, k, False)
+            row_copy(boundary(t + 1, k), t + 1, k).start()
+
+            @pl.when(jnp.logical_and(k == 0, up))
+            def _():
+                i_first(t + 1).start()
+
+            @pl.when(jnp.logical_and(k == n_chunks - 1, down))
+            def _():
+                i_last(t + 1).start()
+
+            return carry
+
+        lax.fori_loop(0, n_chunks, lap, 0)
+        send_k(t + 1)
+        return carry
+
+    lax.fori_loop(0, STEPS - 1, step, 0)
+
+    last = STEPS - 1
+    end = STEPS % 2
+
+    def sums_out(k):
+        return pltpu.make_async_copy(sb.at[:, rows_of(k)], cs_out.at[:, rows_of(k)], out_sem.at[0, k])
+
+    def field_out(k):
+        return pltpu.make_async_copy(fb.at[end, :, pl.ds(1 + k * chunk, chunk)], f_out.at[:, rows_of(k)], out_sem.at[1, k])
+
+    def total_copy(k):
+        return row_copy(sb.at[nj - 1, rows_of(k)], STEPS, k)
+
+    def last_lap(k, carry):
+        step_chunk(last, k, True)
+
+        @pl.when(r == 0)
+        def _():
+            total_copy(k).start()
+            sums_out(k).start()
+
+        field_out(k).start()
+        return carry
+
+    lax.fori_loop(0, n_chunks, last_lap, 0)
+
+    def drain(k, carry):
+        row_copy(boundary(last, k), last, k).wait_send()
+        field_out(k).wait()
+        return carry
+
+    lax.fori_loop(0, n_chunks, drain, 0)
+
+    @pl.when(up)
+    def _():
+        i_first(last).wait_send()
+
+    @pl.when(down)
+    def _():
+        i_last(last).wait_send()
+
+    def drain_k(t, carry):
+        @pl.when(left)
+        def _():
+            k_first(t).wait_send()
+
+        @pl.when(right)
+        def _():
+            k_last(t).wait_send()
+
+        return carry
+
+    lax.fori_loop(0, STEPS, drain_k, 0)
+
+    @pl.when(r == 0)
+    def _():
+        def finish(k, carry):
+            total_copy(k).wait_send()
+            sums_out(k).wait()
+            return carry
+
+        lax.fori_loop(0, n_chunks, finish, 0)
+
+    @pl.when(r == 1)
+    def _():
+        def finish(k, carry):
+            total_copy(k).wait_recv()
+
+            def add_row(n, carry):
+                i = k * chunk + n
+                below = rhalo[STEPS, i]
+                for j in range(nj):
+                    sb[j, i] = sb[j, i] + below
+                return carry
+
+            lax.fori_loop(0, chunk, add_row, 0)
+            sums_out(k).start()
+            return carry
+
+        lax.fori_loop(0, n_chunks, finish, 0)
+
+        def flush(k, carry):
+            sums_out(k).wait()
+            return carry
+
+        lax.fori_loop(0, n_chunks, flush, 0)
+
+
+def fused(counts, field_values, mobility, source):
+    nj, ni, nk, lanes = field_values.shape
+    chunk = math.gcd(ni, 8)
+    n_chunks = ni // chunk
+    shape = jax.ShapeDtypeStruct(field_values.shape, jnp.float32)
+    dma = pltpu.SemaphoreType.DMA
+    return pl.pallas_call(
+        functools.partial(kernel, counts, chunk),
+        out_shape=(shape, shape),
+        in_specs=[pl.BlockSpec(memory_space=pl.ANY)] * 3,
+        out_specs=[pl.BlockSpec(memory_space=pl.ANY)] * 2,
+        scratch_shapes=[
+            pltpu.VMEM((2, nj, ni + 2, nk, lanes), jnp.float32),
+            pltpu.VMEM((nj, ni, nk, lanes), jnp.float32),
+            pltpu.VMEM((nj, ni, nk, lanes), jnp.float32),
+            pltpu.VMEM((STEPS + 1, ni, nk, lanes), jnp.float32),
+            pltpu.VMEM((STEPS, 2, nj, ni, lanes), jnp.float32),
+            pltpu.VMEM((STEPS, 2, nj, ni, lanes), jnp.float32),
+            dma((STEPS + 1, n_chunks)),
+            dma((STEPS + 1, n_chunks)),
+            dma((STEPS, 2)),
+            dma((STEPS, 2)),
+            dma((STEPS, 2)),
+            dma((STEPS, 2)),
+            dma((3,)),
+            dma((2, n_chunks)),
+        ],
+        compiler_params=pltpu.CompilerParams(collective_id=0, has_side_effects=True, vmem_limit_bytes=56 * 1024 * 1024),
+    )(field_values, mobility, source)
 
 
 def padded_2(array, sides, width):
@@ -74,4 +397,8 @@
         P("rows", "cols", "slabs", None),
     )
     out_specs = (P("rows", "cols", "slabs", None), P("rows", "cols", "slabs", None))
-    return jax.shard_map(local, mesh=mesh, in_specs=in_specs, out_specs=out_specs, check_vma=False)
+    if mesh.shape["rows"] == 2:
+        body = functools.partial(fused, tuple(mesh.shape[name] for name in ("rows", "cols", "slabs")))
+    else:
+        body = local
+    return jax.shard_map(body, mesh=mesh, in_specs=in_specs, out_specs=out_specs, check_vma=False)

time: 499 us -> 243 us (0.49)
  waiting for transfers between devices: 275 us -> 0 us
  Pallas kernels: 0 us -> 230 us
  other arithmetic: 136 us -> 0 us
  starting transfers between devices: 52.5 us -> 0 us
  between operations: 14.6 us -> 0.65 us
  local copies, waits for them, and re-layouts: 20.1 us -> 12 us
    pallas_call x0 -> x1, Pallas kernels: none -> 230 us  [fused(): pl.pallas_call(functools.partial(kernel, counts, chunk), out_shape=(shape...]
    ppermute x24 -> x0, waiting for transfers between devices: 218 us -> none  [the longest x12 174 us: padded_2(): before = lax.ppermute(last, axis, up)]
    add x4 -> x0, other arithmetic: 113 us -> none  [one_step(): return middle + mobility * spread + source]
    all_gather x1 -> x0, waiting for transfers between devices: 57 us -> none  [prefix(): everything = lax.all_gather(array, axis)]
    ppermute x24 -> x0, starting transfers between devices: 52.5 us -> none  [the longest x12 36.6 us: padded_2(): before = lax.ppermute(last, axis, up)]
    slice x14 -> x0, local copies, waits for them, and re-layouts: 13.4 us -> none  [the longest x8 6 us: padded_2(): last = lax.slice_in_dim(array, length - width, length, axis=dim)]
    div x1 -> x0, other arithmetic: 8.78 us -> none  [local(): (here + below) / (field_values.shape[0] * lax.axis_size('rows'))]
    unnamed x22 -> x4, local copies, waits for them, and re-layouts: 3.25 us -> 12 us
  transfers between devices with their start and end apart: 25 -> 0, of which waited for: 21 -> 0; matrix products, arithmetic and copies ran while one was open for 1% -> 0% of each run, Pallas kernels for 0% -> 0%
where the time goes in v1:
time: 243 us; the launch traced here: 242 us
  Pallas kernels  230 us (95%)
  local copies, waits for them, and re-layouts  12 us (5%)
    pallas_call x1, Pallas kernels, fused(): pl.pallas_call(functools.partial(kernel, counts, chunk), out_shape=(shape...  230 us
    unnamed x4, local copies, waits for them, and re-layouts  12 us

profile of v1, /device:TPU:0, one launch (start us, length us, event | category | flops | bytes accessed | tf_op | source)
XLA Modules:
  0.0 242.3 jit_solution(3245490569381618388)
XLA Ops:
  0.6 229.6 %shard_map.50 = (f32[4,64,64,128]{3,2,1,0:T(8,128)}, f32[4,64,64,128]{3,2,1,0:T(8,128)}) custom-call(f32[4,64,64,128]{3,2,1,0:T(8,128)} %f_in.1, f32[4,64,64,128]{3,2,1,0:T(8,128)} %m_in.1, f32[4,64,64,128]{3,2,1,0:T(8,128)} %s_in.1), custom_call_target="tpu_custom_call" | custom-call | tf_op jit(solution)/shard_map/pallas_call | solution.py:307
  230.3 0.0 copy-start
  230.3 8.6 %copy.7 = f32[4,64,64,128]{3,2,1,0:T(8,128)} copy(f32[4,64,64,128]{3,2,1,0:T(8,128)} %get-tuple-element.4) | data formatting | bytes 16777216
  238.9 0.0 copy-done
  238.9 3.4 %copy.8 = f32[4,64,64,128]{3,2,1,0:T(8,128)} copy(f32[4,64,64,128]{3,2,1,0:T(8,128)S(1)} %copy-done) | data formatting | bytes 16777216
Async XLA Ops:
  230.3 8.6 %copy-start = (f32[4,64,64,128]{3,2,1,0:T(8,128)S(1)}, f32[4,64,64,128]{3,2,1,0:T(8,128)}, u32[]{:S(2)}) copy-start(f32[4,64,64,128]{3,2,1,0:T(8,128)} %get-tuple-element.5) | copy-start | bytes 25165828

commit v2 on v1

--- a/solution.py
+++ b/solution.py
@@ -12,7 +12,7 @@
 MESH = pl.DeviceIdType.MESH
 
 
-def kernel(counts, chunk, f_in, m_in, s_in, cs_out, f_out, fb, mb, sb, rhalo, khalo, ksend, row_send, row_recv, i_send, i_recv, k_send, k_recv, load_sem, out_sem):
+def kernel(counts, chunk, f_in, m_in, s_in, sb, mb, fb, rhalo, khalo, ksend, row_send, row_recv, i_send, i_recv, k_send, k_recv, load_sem):
     n_rows, n_cols, n_slabs = counts
     nj, ni, nk, lanes = f_in.shape
     n_chunks = ni // chunk
@@ -179,11 +179,12 @@
                 k_after = jnp.where(at_last, khalo[t, 1, j, pl.ds(i, 1), :], pltpu.roll(x, nk - 1, 0))
                 spread = before + after + fb[p, j, i] + fb[p, j, i + 2] + k_before + k_after - 6.0 * x
                 new = x + mb[j, i] * spread + sb[j, i]
-                fb[q, j, i + 1] = new
                 if final:
+                    mb[j, i] = new
                     total = new if total is None else total + new
                     sb[j, i] = total * scale
                 else:
+                    fb[q, j, i + 1] = new
                     ksend[t + 1, 0, j, pl.ds(i, 1), :] = new[0:1]
                     ksend[t + 1, 1, j, pl.ds(i, 1), :] = new[nk - 1 : nk]
             return carry
@@ -212,13 +213,6 @@
     lax.fori_loop(0, STEPS - 1, step, 0)
 
     last = STEPS - 1
-    end = STEPS % 2
-
-    def sums_out(k):
-        return pltpu.make_async_copy(sb.at[:, rows_of(k)], cs_out.at[:, rows_of(k)], out_sem.at[0, k])
-
-    def field_out(k):
-        return pltpu.make_async_copy(fb.at[end, :, pl.ds(1 + k * chunk, chunk)], f_out.at[:, rows_of(k)], out_sem.at[1, k])
 
     def total_copy(k):
         return row_copy(sb.at[nj - 1, rows_of(k)], STEPS, k)
@@ -229,16 +223,13 @@
         @pl.when(r == 0)
         def _():
             total_copy(k).start()
-            sums_out(k).start()
-
-        field_out(k).start()
+
         return carry
 
     lax.fori_loop(0, n_chunks, last_lap, 0)
 
     def drain(k, carry):
         row_copy(boundary(last, k), last, k).wait_send()
-        field_out(k).wait()
         return carry
 
     lax.fori_loop(0, n_chunks, drain, 0)
@@ -268,7 +259,6 @@
     def _():
         def finish(k, carry):
             total_copy(k).wait_send()
-            sums_out(k).wait()
             return carry
 
         lax.fori_loop(0, n_chunks, finish, 0)
@@ -286,33 +276,35 @@
                 return carry
 
             lax.fori_loop(0, chunk, add_row, 0)
-            sums_out(k).start()
             return carry
 
         lax.fori_loop(0, n_chunks, finish, 0)
 
-        def flush(k, carry):
-            sums_out(k).wait()
-            return carry
-
-        lax.fori_loop(0, n_chunks, flush, 0)
+
+def flush(sums, field, sums_out, field_out, sem):
+    copies = []
+    for side, (src, dst) in enumerate(((sums, sums_out), (field, field_out))):
+        for j in range(src.shape[0]):
+            copies.append(pltpu.make_async_copy(src.at[j], dst.at[j], sem.at[side, j]))
+    for copy in copies:
+        copy.start()
+    for copy in copies:
+        copy.wait()
 
 
 def fused(counts, field_values, mobility, source):
     nj, ni, nk, lanes = field_values.shape
     chunk = math.gcd(ni, 8)
     n_chunks = ni // chunk
-    shape = jax.ShapeDtypeStruct(field_values.shape, jnp.float32)
+    shape = pltpu.VMEM(field_values.shape, jnp.float32)
     dma = pltpu.SemaphoreType.DMA
-    return pl.pallas_call(
+    sums, field = pl.pallas_call(
         functools.partial(kernel, counts, chunk),
         out_shape=(shape, shape),
         in_specs=[pl.BlockSpec(memory_space=pl.ANY)] * 3,
-        out_specs=[pl.BlockSpec(memory_space=pl.ANY)] * 2,
+        out_specs=[pl.BlockSpec(memory_space=pltpu.VMEM)] * 2,
         scratch_shapes=[
             pltpu.VMEM((2, nj, ni + 2, nk, lanes), jnp.float32),
-            pltpu.VMEM((nj, ni, nk, lanes), jnp.float32),
-            pltpu.VMEM((nj, ni, nk, lanes), jnp.float32),
             pltpu.VMEM((STEPS + 1, ni, nk, lanes), jnp.float32),
             pltpu.VMEM((STEPS, 2, nj, ni, lanes), jnp.float32),
             pltpu.VMEM((STEPS, 2, nj, ni, lanes), jnp.float32),
@@ -323,10 +315,18 @@
             dma((STEPS, 2)),
             dma((STEPS, 2)),
             dma((3,)),
-            dma((2, n_chunks)),
         ],
-        compiler_params=pltpu.CompilerParams(collective_id=0, has_side_effects=True, vmem_limit_bytes=56 * 1024 * 1024),
+        compiler_params=pltpu.CompilerParams(collective_id=0, has_side_effects=True, vmem_limit_bytes=32 * 1024 * 1024),
     )(field_values, mobility, source)
+    result = jax.ShapeDtypeStruct(field_values.shape, jnp.float32)
+    return pl.pallas_call(
+        flush,
+        out_shape=(result, result),
+        in_specs=[pl.BlockSpec(memory_space=pltpu.VMEM)] * 2,
+        out_specs=[pl.BlockSpec(memory_space=pl.ANY)] * 2,
+        scratch_shapes=[dma((2, nj))],
+        compiler_params=pltpu.CompilerParams(vmem_limit_bytes=18 * 1024 * 1024),
+    )(sums, field)
 
 
 def padded_2(array, sides, width):

time: 243 us -> 236 us (0.971)
  local copies, waits for them, and re-layouts: 12 us -> 0 us
  Pallas kernels: 230 us -> 235 us
    unnamed x4 -> x0, local copies, waits for them, and re-layouts: 12 us -> none
    pallas_call x0 -> x1, Pallas kernels: none -> 5.93 us  [fused(): pl.pallas_call(flush, out_shape=(result, result), in_specs=[pl.BlockSpec(...]
where the time goes in v2:
time: 236 us
  Pallas kernels  235 us (100%)
    pallas_call x1, Pallas kernels, fused(): pl.pallas_call(functools.partial(kernel, counts, chunk), out_shape=(shape...  229 us
    pallas_call x1, Pallas kernels, fused(): pl.pallas_call(flush, out_shape=(result, result), in_specs=[pl.BlockSpec(...  5.93 us

profile of v2, /device:TPU:0, one launch (start us, length us, event | category | flops | bytes accessed | tf_op | source)
XLA Modules:
  0.0 236.1 jit_solution(7425062397589865575)
XLA Ops:
  0.6 229.5 %shard_map.50 = (f32[4,64,64,128]{3,2,1,0:T(8,128)S(1)}, f32[4,64,64,128]{3,2,1,0:T(8,128)S(1)}) custom-call(f32[4,64,64,128]{3,2,1,0:T(8,128)} %f_in.1, f32[4,64,64,128]{3,2,1,0:T(8,128)} %m_in.1, f32[4,64,64,128]{3,2,1,0:T(8,128)} %s_in.1), custom_call_target="tpu_custom_call" | custom-call | tf_op jit(solution)/shard_map/pallas_call | solution.py:301
  230.1 5.9 %shard_map.51 = (f32[4,64,64,128]{3,2,1,0:T(8,128)}, f32[4,64,64,128]{3,2,1,0:T(8,128)}) custom-call(f32[4,64,64,128]{3,2,1,0:T(8,128)S(1)} %get-tuple-element.4.sums, f32[4,64,64,128]{3,2,1,0:T(8,128)S(1)} %get-tuple-element.5.field), custom_call_target="tpu_custom_call" | custom-call | tf_op jit(solution)/shard_map/pallas_call | solution.py:322
